TPU v7x, 16 devices: a whole 2x2x2 slice. The times are simulated.
16 devices in a mesh: stage: 4 (over z, y), tp: 4 (over x, core).
Axes of the slice: x: 2, y: 2, z: 2, core: 2. Of those that a mesh axis runs over, the one named last changes fastest.
Arguments:
- x: bfloat16 [8, 1024, 2560], P(None, 'tp')
- g: bfloat16 [4, 2, 2560], P('stage')
- w1: bfloat16 [4, 2, 2560, 10240], P('stage', None, None, 'tp')
- w2: bfloat16 [4, 2, 10240, 2560], P('stage', None, 'tp')
Outputs:
- output: bfloat16 [4, 8, 1024, 2560], P('stage', None, 'tp')
All inputs are finite; a program needn't handle non-finite values.
Results may differ from a plain program's by a relative error of at most 0.02.
Values are sent between devices in bfloat16 or wider.
A program may use at most 1 GiB of HBM per device.

v0:
```python
import jax
import jax.numpy as jnp
from jax import lax
from jax.sharding import PartitionSpec as P

EPS = 1e-5


def _ln(y, g):
    yf = y.astype(jnp.float32)
    mu = jnp.mean(yf, axis=-1, keepdims=True)
    var = jnp.mean(jnp.square(yf - mu), axis=-1, keepdims=True)
    return ((yf - mu) * lax.rsqrt(var + EPS) * g.astype(jnp.float32)).astype(jnp.bfloat16)


def _block(y, g, w1, w2):
    h = lax.all_gather(_ln(y, g), 'tp', axis=0, tiled=True)
    a = jax.nn.gelu(jnp.dot(h, w1, preferred_element_type=jnp.float32)).astype(jnp.bfloat16)
    p = jnp.dot(a, w2, preferred_element_type=jnp.float32).astype(jnp.bfloat16)
    r = lax.psum_scatter(p, 'tp', scatter_dimension=0, tiled=True)
    return (y.astype(jnp.float32) + r.astype(jnp.float32)).astype(jnp.bfloat16)


def solution(mesh):
    S = mesh.shape['stage']
    fwd = [(i, i + 1) for i in range(S - 1)]

    def local(x, g, w1, w2):
        s = lax.axis_index('stage')
        M = x.shape[0]
        nb = g.shape[1]
        out = jnp.zeros_like(x)
        recv = jnp.zeros_like(x[0])
        for k in range(M + S - 1):
            y = jnp.where(s == 0, x[min(k, M - 1)], recv)
            for b in range(nb):
                y = _block(y, g[0, b], w1[0, b], w2[0, b])
            m = k - s
            mc = jnp.clip(m, 0, M - 1)
            old = lax.dynamic_index_in_dim(out, mc, 0, keepdims=False)
            out = lax.dynamic_update_index_in_dim(out, jnp.where((m >= 0) & (m < M), y, old), mc, 0)
            if k < M + S - 2:
                recv = lax.ppermute(y, 'stage', fwd)
        return out[None]

    return jax.shard_map(
        local, mesh=mesh,
        in_specs=(P(None, 'tp', None), P('stage', None, None),
                  P('stage', None, None, 'tp'), P('stage', None, 'tp', None)),
        out_specs=P('stage', None, 'tp', None), check_vma=False)
```

profile of v0, /device:TPU:12, one launch (start us, length us, event | category | flops | bytes accessed | tf_op | source)
XLA Modules:
  0.0 3173.2 jit_solution(9110036074202855967)
XLA Ops:
  13.9 39.5 %all-gather.23.cloned.1.call-done = bf16[1024,2560]{1,0:T(8,128)(2,1)} async-done(((bf16[256,2560]{1,0:T(8,128)(2,1)}), bf16[1024,2560]{1,0:T(8,128)(2,1)}) %all-gather.23.cloned.1.call-update) | async-done | bytes 5242896 | tf_op jit(solution)/shard_map/all_gather | solution.py:17
  91.4 46.5 %reduce-scatter.23.cloned.1.call-done = bf16[256,2560]{1,0:T(8,128)(2,1)} async-done(((bf16[1024,2560]{1,0:T(8,128)(2,1)}), bf16[256,2560]{1,0:T(8,128)(2,1)}) %reduce-scatter.23.cloned.1.call-update) | async-done | bytes 1310736 | tf_op jit(solution)/shard_map/reduce_scatter | solution.py:20
  307.8 38.8 %all-gather.27.cloned.1.call-done = bf16[1024,2560]{1,0:T(8,128)(2,1)} async-done(((bf16[256,2560]{1,0:T(8,128)(2,1)}), bf16[1024,2560]{1,0:T(8,128)(2,1)}) %all-gather.27.cloned.1.call-update) | async-done | bytes 5242896 | tf_op jit(solution)/shard_map/all_gather | solution.py:17
  384.5 46.7 %reduce-scatter.27.cloned.1.call-done = bf16[256,2560]{1,0:T(8,128)(2,1)} async-done(((bf16[1024,2560]{1,0:T(8,128)(2,1)}), bf16[256,2560]{1,0:T(8,128)(2,1)}) %reduce-scatter.27.cloned.1.call-update) | async-done | bytes 1310736 | tf_op jit(solution)/shard_map/reduce_scatter | solution.py:20
  513.0 45.3 %reduce-scatter.29.cloned.1.call-done = bf16[256,2560]{1,0:T(8,128)(2,1)} async-done(((bf16[1024,2560]{1,0:T(8,128)(2,1)}), bf16[256,2560]{1,0:T(8,128)(2,1)}) %reduce-scatter.29.cloned.1.call-update) | async-done | bytes 1310736 | tf_op jit(solution)/shard_map/reduce_scatter | solution.py:20
  597.4 38.6 %all-gather.31.cloned.1.call-done = bf16[1024,2560]{1,0:T(8,128)(2,1)} async-done(((bf16[256,2560]{1,0:T(8,128)(2,1)}), bf16[1024,2560]{1,0:T(8,128)(2,1)}) %all-gather.31.cloned.1.call-update) | async-done | bytes 5242896 | tf_op jit(solution)/shard_map/all_gather | solution.py:17
  673.9 46.7 %reduce-scatter.31.cloned.1.call-done = bf16[256,2560]{1,0:T(8,128)(2,1)} async-done(((bf16[1024,2560]{1,0:T(8,128)(2,1)}), bf16[256,2560]{1,0:T(8,128)(2,1)}) %reduce-scatter.31.cloned.1.call-update) | async-done | bytes 1310736 | tf_op jit(solution)/shard_map/reduce_scatter | solution.py:20
  802.4 45.3 %reduce-scatter.33.cloned.1.call-done = bf16[256,2560]{1,0:T(8,128)(2,1)} async-done(((bf16[1024,2560]{1,0:T(8,128)(2,1)}), bf16[256,2560]{1,0:T(8,128)(2,1)}) %reduce-scatter.33.cloned.1.call-update) | async-done | bytes 1310736 | tf_op jit(solution)/shard_map/reduce_scatter | solution.py:20
  963.3 46.7 %reduce-scatter.35.cloned.1.call-done = bf16[256,2560]{1,0:T(8,128)(2,1)} async-done(((bf16[1024,2560]{1,0:T(8,128)(2,1)}), bf16[256,2560]{1,0:T(8,128)(2,1)}) %reduce-scatter.35.cloned.1.call-update) | async-done | bytes 1310736 | tf_op jit(solution)/shard_map/reduce_scatter | solution.py:20
  1091.8 45.3 %reduce-scatter.37.cloned.1.call-done = bf16[256,2560]{1,0:T(8,128)(2,1)} async-done(((bf16[1024,2560]{1,0:T(8,128)(2,1)}), bf16[256,2560]{1,0:T(8,128)(2,1)}) %reduce-scatter.37.cloned.1.call-update) | async-done | bytes 1310736 | tf_op jit(solution)/shard_map/reduce_scatter | solution.py:20
  1252.7 46.7 %reduce-scatter.39.cloned.1.call-done = bf16[256,2560]{1,0:T(8,128)(2,1)} async-done(((bf16[1024,2560]{1,0:T(8,128)(2,1)}), bf16[256,2560]{1,0:T(8,128)(2,1)}) %reduce-scatter.39.cloned.1.call-update) | async-done | bytes 1310736 | tf_op jit(solution)/shard_map/reduce_scatter | solution.py:20
  1381.2 45.3 %reduce-scatter.41.cloned.1.call-done = bf16[256,2560]{1,0:T(8,128)(2,1)} async-done(((bf16[1024,2560]{1,0:T(8,128)(2,1)}), bf16[256,2560]{1,0:T(8,128)(2,1)}) %reduce-scatter.41.cloned.1.call-update) | async-done | bytes 1310736 | tf_op jit(solution)/shard_map/reduce_scatter | solution.py:20
  1465.6 38.6 %all-gather.43.cloned.1.call-done = bf16[1024,2560]{1,0:T(8,128)(2,1)} async-done(((bf16[256,2560]{1,0:T(8,128)(2,1)}), bf16[1024,2560]{1,0:T(8,128)(2,1)}) %all-gather.43.cloned.1.call-update) | async-done | bytes 5242896 | tf_op jit(solution)/shard_map/all_gather | solution.py:17
  1542.1 46.7 %reduce-scatter.43.cloned.1.call-done = bf16[256,2560]{1,0:T(8,128)(2,1)} async-done(((bf16[1024,2560]{1,0:T(8,128)(2,1)}), bf16[256,2560]{1,0:T(8,128)(2,1)}) %reduce-scatter.43.cloned.1.call-update) | async-done | bytes 1310736 | tf_op jit(solution)/shard_map/reduce_scatter | solution.py:20
  1670.6 45.3 %reduce-scatter.45.cloned.1.call-done = bf16[256,2560]{1,0:T(8,128)(2,1)} async-done(((bf16[1024,2560]{1,0:T(8,128)(2,1)}), bf16[256,2560]{1,0:T(8,128)(2,1)}) %reduce-scatter.45.cloned.1.call-update) | async-done | bytes 1310736 | tf_op jit(solution)/shard_map/reduce_scatter | solution.py:20
  1831.5 46.7 %reduce-scatter.47.cloned.1.call-done = bf16[256,2560]{1,0:T(8,128)(2,1)} async-done(((bf16[1024,2560]{1,0:T(8,128)(2,1)}), bf16[256,2560]{1,0:T(8,128)(2,1)}) %reduce-scatter.47.cloned.1.call-update) | async-done | bytes 1310736 | tf_op jit(solution)/shard_map/reduce_scatter | solution.py:20
  1960.0 45.3 %reduce-scatter.49.cloned.1.call-done = bf16[256,2560]{1,0:T(8,128)(2,1)} async-done(((bf16[1024,2560]{1,0:T(8,128)(2,1)}), bf16[256,2560]{1,0:T(8,128)(2,1)}) %reduce-scatter.49.cloned.1.call-update) | async-done | bytes 1310736 | tf_op jit(solution)/shard_map/reduce_scatter | solution.py:20
  2120.9 46.7 %reduce-scatter.51.cloned.1.call-done = bf16[256,2560]{1,0:T(8,128)(2,1)} async-done(((bf16[1024,2560]{1,0:T(8,128)(2,1)}), bf16[256,2560]{1,0:T(8,128)(2,1)}) %reduce-scatter.51.cloned.1.call-update) | async-done | bytes 1310736 | tf_op jit(solution)/shard_map/reduce_scatter | solution.py:20
  2249.4 45.3 %reduce-scatter.53.cloned.1.call-done = bf16[256,2560]{1,0:T(8,128)(2,1)} async-done(((bf16[1024,2560]{1,0:T(8,128)(2,1)}), bf16[256,2560]{1,0:T(8,128)(2,1)}) %reduce-scatter.53.cloned.1.call-update) | async-done | bytes 1310736 | tf_op jit(solution)/shard_map/reduce_scatter | solution.py:20
  2410.3 46.7 %reduce-scatter.55.cloned.1.call-done = bf16[256,2560]{1,0:T(8,128)(2,1)} async-done(((bf16[1024,2560]{1,0:T(8,128)(2,1)}), bf16[256,2560]{1,0:T(8,128)(2,1)}) %reduce-scatter.55.cloned.1.call-update) | async-done | bytes 1310736 | tf_op jit(solution)/shard_map/reduce_scatter | solution.py:20
  2538.8 45.3 %reduce-scatter.57.cloned.1.call-done = bf16[256,2560]{1,0:T(8,128)(2,1)} async-done(((bf16[1024,2560]{1,0:T(8,128)(2,1)}), bf16[256,2560]{1,0:T(8,128)(2,1)}) %reduce-scatter.57.cloned.1.call-update) | async-done | bytes 1310736 | tf_op jit(solution)/shard_map/reduce_scatter | solution.py:20
  2699.8 46.7 %reduce-scatter.59.cloned.1.call-done = bf16[256,2560]{1,0:T(8,128)(2,1)} async-done(((bf16[1024,2560]{1,0:T(8,128)(2,1)}), bf16[256,2560]{1,0:T(8,128)(2,1)}) %reduce-scatter.59.cloned.1.call-update) | async-done | bytes 1310736 | tf_op jit(solution)/shard_map/reduce_scatter | solution.py:20
  2828.3 45.3 %reduce-scatter.61.cloned.1.call-done = bf16[256,2560]{1,0:T(8,128)(2,1)} async-done(((bf16[1024,2560]{1,0:T(8,128)(2,1)}), bf16[256,2560]{1,0:T(8,128)(2,1)}) %reduce-scatter.61.cloned.1.call-update) | async-done | bytes 1310736 | tf_op jit(solution)/shard_map/reduce_scatter | solution.py:20
  2989.2 46.7 %reduce-scatter.63.cloned.1.call-done = bf16[256,2560]{1,0:T(8,128)(2,1)} async-done(((bf16[1024,2560]{1,0:T(8,128)(2,1)}), bf16[256,2560]{1,0:T(8,128)(2,1)}) %reduce-scatter.63.cloned.1.call-update) | async-done | bytes 1310736 | tf_op jit(solution)/shard_map/reduce_scatter | solution.py:20
  (307 shorter events, 2081.5 us)
Async XLA Ops:
  13.8 124.1 %reduce-scatter.23.cloned.1.call-start = ((), (), s32[]{:S(2)}) async-start(), calls=%async_computation.23 | async-start | bytes 6553600 | tf_op jit(solution)/shard_map/reduce_scatter | solution.py:20
  218.6 128.0 %all-gather.27.cloned.1.call-start = ((), (), s32[]{:S(2)}) async-start(), calls=%async_computation.26 | async-start | bytes 6553600 | tf_op jit(solution)/shard_map/all_gather | solution.py:17
  307.8 123.4 %reduce-scatter.27.cloned.1.call-start = ((), (), s32[]{:S(2)}) async-start(), calls=%async_computation.27 | async-start | bytes 6553600 | tf_op jit(solution)/shard_map/reduce_scatter | solution.py:20
  511.5 124.5 %all-gather.31.cloned.1.call-start = ((), (), s32[]{:S(2)}) async-start(), calls=%async_computation.30 | async-start | bytes 6553600 | tf_op jit(solution)/shard_map/all_gather | solution.py:17
  597.2 123.4 %reduce-scatter.31.cloned.1.call-start = ((), (), s32[]{:S(2)}) async-start(), calls=%async_computation.31 | async-start | bytes 6553600 | tf_op jit(solution)/shard_map/reduce_scatter | solution.py:20
  800.9 124.5 %all-gather.35.cloned.1.call-start = ((), (), s32[]{:S(2)}) async-start(), calls=%async_computation.34 | async-start | bytes 6553600 | tf_op jit(solution)/shard_map/all_gather | solution.py:17
  886.6 123.4 %reduce-scatter.35.cloned.1.call-start = ((), (), s32[]{:S(2)}) async-start(), calls=%async_computation.35 | async-start | bytes 6553600 | tf_op jit(solution)/shard_map/reduce_scatter | solution.py:20
  1090.3 124.6 %all-gather.39.cloned.1.call-start = ((), (), s32[]{:S(2)}) async-start(), calls=%async_computation.38 | async-start | bytes 6553600 | tf_op jit(solution)/shard_map/all_gather | solution.py:17
  1176.0 123.4 %reduce-scatter.39.cloned.1.call-start = ((), (), s32[]{:S(2)}) async-start(), calls=%async_computation.39 | async-start | bytes 6553600 | tf_op jit(solution)/shard_map/reduce_scatter | solution.py:20
  1379.7 124.6 %all-gather.43.cloned.1.call-start = ((), (), s32[]{:S(2)}) async-start(), calls=%async_computation.42 | async-start | bytes 6553600 | tf_op jit(solution)/shard_map/all_gather | solution.py:17
  1465.4 123.4 %reduce-scatter.43.cloned.1.call-start = ((), (), s32[]{:S(2)}) async-start(), calls=%async_computation.43 | async-start | bytes 6553600 | tf_op jit(solution)/shard_map/reduce_scatter | solution.py:20
  1669.2 124.5 %all-gather.47.cloned.1.call-start = ((), (), s32[]{:S(2)}) async-start(), calls=%async_computation.46 | async-start | bytes 6553600 | tf_op jit(solution)/shard_map/all_gather | solution.py:17
  1754.9 123.4 %reduce-scatter.47.cloned.1.call-start = ((), (), s32[]{:S(2)}) async-start(), calls=%async_computation.47 | async-start | bytes 6553600 | tf_op jit(solution)/shard_map/reduce_scatter | solution.py:20
  1882.1 123.2 %reduce-scatter.49.cloned.1.call-start = ((), (), s32[]{:S(2)}) async-start(), calls=%async_computation.49 | async-start | bytes 6553600 | tf_op jit(solution)/shard_map/reduce_scatter | solution.py:20
  1958.6 124.6 %all-gather.51.cloned.1.call-start = ((), (), s32[]{:S(2)}) async-start(), calls=%async_computation.50 | async-start | bytes 6553600 | tf_op jit(solution)/shard_map/all_gather | solution.py:17
  2044.2 123.4 %reduce-scatter.51.cloned.1.call-start = ((), (), s32[]{:S(2)}) async-start(), calls=%async_computation.51 | async-start | bytes 6553600 | tf_op jit(solution)/shard_map/reduce_scatter | solution.py:20
  2248.0 124.5 %all-gather.55.cloned.1.call-start = ((), (), s32[]{:S(2)}) async-start(), calls=%async_computation.54 | async-start | bytes 6553600 | tf_op jit(solution)/shard_map/all_gather | solution.py:17
  2333.7 123.4 %reduce-scatter.55.cloned.1.call-start = ((), (), s32[]{:S(2)}) async-start(), calls=%async_computation.55 | async-start | bytes 6553600 | tf_op jit(solution)/shard_map/reduce_scatter | solution.py:20
  2460.9 123.2 %reduce-scatter.57.cloned.1.call-start = ((), (), s32[]{:S(2)}) async-start(), calls=%async_computation.57 | async-start | bytes 6553600 | tf_op jit(solution)/shard_map/reduce_scatter | solution.py:20
  2537.3 124.7 %all-gather.59.cloned.1.call-start = ((), (), s32[]{:S(2)}) async-start(), calls=%async_computation.58 | async-start | bytes 6553600 | tf_op jit(solution)/shard_map/all_gather | solution.py:17
  2623.0 123.6 %reduce-scatter.59.cloned.1.call-start = ((), (), s32[]{:S(2)}) async-start(), calls=%async_computation.59 | async-start | bytes 6553600 | tf_op jit(solution)/shard_map/reduce_scatter | solution.py:20
  2826.9 124.5 %all-gather.63.cloned.1.call-start = ((), (), s32[]{:S(2)}) async-start(), calls=%async_computation.62 | async-start | bytes 6553600 | tf_op jit(solution)/shard_map/all_gather | solution.py:17
  2912.7 123.3 %reduce-scatter.63.cloned.1.call-start = ((), (), s32[]{:S(2)}) async-start(), calls=%async_computation.63 | async-start | bytes 6553600 | tf_op jit(solution)/shard_map/reduce_scatter | solution.py:20
  3039.8 123.2 %reduce-scatter.65.cloned.1.call-start = ((), (), s32[]{:S(2)}) async-start(), calls=%async_computation.65 | async-start | bytes 6553600 | tf_op jit(solution)/shard_map/reduce_scatter | solution.py:20
  (31 other events, 2341.2 us)
Sparse Core Ops, SparseCore 0:
  13.9 39.3 all-gather.22
  91.2 46.6 reduce-scatter.22
  218.7 46.6 reduce-scatter.24
  384.6 46.6 reduce-scatter.26
  511.6 46.5 reduce-scatter.28
  673.9 46.6 reduce-scatter.30
  801.0 46.5 reduce-scatter.32
  963.3 46.6 reduce-scatter.34
  1090.4 46.5 reduce-scatter.36
  1252.8 46.6 reduce-scatter.38
  1379.8 46.5 reduce-scatter.40
  1542.2 46.6 reduce-scatter.42
  1669.3 46.5 reduce-scatter.44
  1831.6 46.6 reduce-scatter.46
  1958.7 46.5 reduce-scatter.48
  2121.0 46.6 reduce-scatter.50
  2248.1 46.5 reduce-scatter.52
  2410.4 46.5 reduce-scatter.54
  2537.5 46.6 reduce-scatter.56
  2623.1 38.8 all-gather.58
  2699.9 46.6 reduce-scatter.58
  2827.0 46.5 reduce-scatter.60
  2989.3 46.5 reduce-scatter.62
  3116.4 46.5 reduce-scatter.64
  (20 shorter events, 770.0 us)
where the time goes:
time: 3180 us; the launch traced here: 3170 us
  waiting for transfers between devices  2150 us (68%)
  matrix products  831 us (26%)
  other arithmetic  119 us (4%)
    reduce_scatter x22, waiting for transfers between devices, _block(): r = lax.psum_scatter(p, 'tp', scatter_dimension=0, tiled=True)  996 us
    all_gather x22, waiting for transfers between devices, _block(): h = lax.all_gather(_ln(y, g), 'tp', axis=0, tiled=True)  847 us
    dot_general x22, matrix products, _block(): jnp.dot(h, w1, preferred_element_type=jnp.float32)  430 us
    dot_general x22, matrix products, _block(): p = jnp.dot(a, w2, preferred_element_type=jnp.float32).astype(jnp.bfloat16)  401 us
    ppermute x10, waiting for transfers between devices, local(): recv = lax.ppermute(y, 'stage', fwd)  309 us
  transfers between devices with their start and end apart: 54, of which 54 were waited for; matrix products, arithmetic and copies ran while one was open for 1% of the time, Pallas kernels for 0%

commit v1 on v0

v1 whole, which is shorter than its diff:
```python
import functools

import jax
import jax.numpy as jnp
from jax import lax
from jax.experimental import pallas as pl
from jax.experimental.pallas import tpu as pltpu
from jax.sharding import PartitionSpec as P

EPS = 1e-5
Q = 64
TN = 512
YS = 4
RB = 16
MESH = pl.DeviceIdType.MESH


def _kernel(cfg, x_hbm, g_ref, w1_hbm, w2_hbm, y_hbm,
            w1s, w2s, h, a, psend, precv, crossp, own, ssend, srecv, y0, y1, yout,
            w_sem, agp_send, agx_send, fw_send, ag_recv, p_send, p_recv, s_send, s_recv,
            yin_sem, ysend_sem, yhbm_sem, credit):
    S, NB, C, NQ, NT1, NT2, D = cfg
    q = Q
    n = 4 * q
    s = lax.axis_index('stage')
    r = lax.axis_index('tp')
    xr = lax.div(r, 2)
    cr = lax.rem(r, 2)
    partner = xr * 2 + (1 - cr)
    cross = (1 - xr) * 2 + cr

    def rows(i, k=1):
        return pl.ds(i * q, k * q)

    def w1_copy(b, t):
        return pltpu.make_async_copy(w1_hbm.at[b, :, pl.ds(t * TN, TN)], w1s.at[b, t], w_sem.at[0, b, t])

    def w2_copy(b, t):
        return pltpu.make_async_copy(w2_hbm.at[b, :, pl.ds(t * TN, TN)], w2s.at[b, t], w_sem.at[1, b, t])

    def remote(src, dst, ss, rs, **dev):
        return pltpu.make_async_remote_copy(src_ref=src, dst_ref=dst, send_sem=ss, recv_sem=rs,
                                            device_id=dev, device_id_type=MESH)

    def ag_partner(k):
        i = lax.rem(k, 3)
        return remote(h.at[i, rows(0)], h.at[i, rows(2)], agp_send.at[i], ag_recv.at[i, 1], tp=partner)

    def ag_cross(k):
        i = lax.rem(k, 3)
        return remote(h.at[i, rows(0)], h.at[i, rows(1)], agx_send.at[i], ag_recv.at[i, 0], tp=cross)

    def ag_forward(k):
        i = lax.rem(k, 3)
        return remote(h.at[i, rows(1)], h.at[i, rows(3)], fw_send.at[i], ag_recv.at[i, 2], tp=partner)

    def p_copy(k, t):
        return remote(psend.at[t % 2], precv.at[lax.rem(k, 2), t], p_send.at[t % 2],
                      p_recv.at[lax.rem(k, 2), t], tp=partner)

    def s_copy(k, t):
        return remote(ssend.at[lax.rem(k, 2), t], srecv.at[lax.rem(k, 3), t],
                      s_send.at[lax.rem(k, 2), t], s_recv.at[lax.rem(k, 3), t], tp=cross)

    def hbm_rows(ref, c):
        return ref.at[lax.div(c, NQ), pl.ds(pl.multiple_of(lax.rem(c, NQ) * q, q), q)]

    def x_copy(c):
        i = lax.rem(c, YS)
        return pltpu.make_async_copy(hbm_rows(x_hbm, c), y0.at[i], yin_sem.at[i])

    def y_next(c):
        i = lax.rem(c, YS)
        o = lax.rem(c, 2)
        return remote(yout.at[o], y0.at[i], ysend_sem.at[o], yin_sem.at[i], stage=s + 1)

    def y_store(c):
        o = lax.rem(c, 2)
        return pltpu.make_async_copy(yout.at[o], hbm_rows(y_hbm, c), yhbm_sem.at[o])

    def norm(yf, b):
        mu = jnp.mean(yf, axis=-1, keepdims=True)
        d = yf - mu
        var = jnp.mean(jnp.square(d), axis=-1, keepdims=True)
        return (d * lax.rsqrt(var + EPS) * g_ref[b]).astype(jnp.bfloat16)

    def send_h(k):
        ag_cross(k).start()
        ag_partner(k).start()

    def enter(c, k):
        i = lax.rem(c, YS)

        @pl.when(s == 0)
        def _():
            x_copy(c).wait()

            @pl.when(c + 2 < C)
            def _():
                x_copy(c + 2).start()

        @pl.when(s > 0)
        def _():
            y_next(c).wait_recv()

        def body(u, _):
            rr = pl.ds(pl.multiple_of(u * RB, RB), RB)
            h[lax.rem(k, 3), rr] = norm(y0[i, rr].astype(jnp.float32), 0)
            return 0
        lax.fori_loop(0, q // RB, body, 0)
        send_h(k)

    def add_up(j, yref, yi, rr):
        parts = []
        for t in range(NT2):
            yf = yref[yi, rr, t * TN:(t + 1) * TN].astype(jnp.float32)
            parts.append((yf + (own[lax.rem(j, 2), t, rr] + srecv[lax.rem(j, 3), t, rr].astype(jnp.float32))
                          ).astype(jnp.bfloat16))
        return jnp.concatenate(parts, axis=-1)

    def wait_sums(j):
        for t in range(NT2):
            s_copy(j, t).wait()

    def finish0(c, j, k):
        wait_sums(j)
        i = lax.rem(c, YS)
        o = lax.rem(c, 2)

        def body(u, _):
            rr = pl.ds(pl.multiple_of(u * RB, RB), RB)
            y = add_up(j, y0, i, rr)
            y1[o, rr] = y
            h[lax.rem(k, 3), rr] = norm(y.astype(jnp.float32), 1)
            return 0
        lax.fori_loop(0, q // RB, body, 0)
        send_h(k)

        @pl.when((s > 0) & (c + YS < C))
        def _():
            pl.semaphore_signal(credit, inc=1, device_id={'stage': s - 1}, device_id_type=MESH)

    def release(c):
        y_store(c).wait()

        @pl.when(s < S - 1)
        def _():
            y_next(c).wait_send()

    def finish1(c, j):
        o = lax.rem(c, 2)

        @pl.when(c >= 2)
        def _():
            release(c - 2)
        wait_sums(j)

        def body(u, _):
            rr = pl.ds(pl.multiple_of(u * RB, RB), RB)
            yout[o, rr] = add_up(j, y1, o, rr)
            return 0
        lax.fori_loop(0, q // RB, body, 0)

        @pl.when(s < S - 1)
        def _():
            @pl.when(c >= YS)
            def _():
                pl.semaphore_wait(credit, 1)
            y_next(c).start()
        y_store(c).start()

    def compute(k, b, first):
        i = lax.rem(k, 3)
        e = lax.rem(k, 2)
        ag_partner(k).wait()
        ag_cross(k).wait()
        ag_forward(k).start()
        ag_forward(k).wait_recv()
        for t in range(NT1):
            @pl.when(first)
            def _():
                w1_copy(b, t).wait()
            u = jnp.dot(h[i], w1s[b, t], preferred_element_type=jnp.float32)
            a[:, t * TN:(t + 1) * TN] = jax.nn.gelu(u).astype(jnp.bfloat16)
        ag_forward(k).wait_send()

        def combine(t):
            p_copy(k, t).wait()
            own[e, t] = own[e, t] + precv[e, t, 0:q].astype(jnp.float32)
            ssend[e, t] = (crossp[t % 2] + precv[e, t, q:2 * q].astype(jnp.float32)).astype(jnp.bfloat16)
            s_copy(k, t).start()

        for t in range(NT2):
            @pl.when(first)
            def _():
                w2_copy(b, t).wait()
            p = jnp.dot(a[...], w2s[b, t], preferred_element_type=jnp.float32)
            psend[t % 2] = p[2 * q:].astype(jnp.bfloat16)
            own[e, t] = p[0:q]
            crossp[t % 2] = p[q:2 * q]
            p_copy(k, t).start()
            if t > 0:
                combine(t - 1)
        combine(NT2 - 1)

    @pl.when(s == 0)
    def _():
        x_copy(0).start()
        x_copy(1).start()
    for b in range(NB):
        for t in range(NT1):
            w1_copy(b, t).start()
        for t in range(NT2):
            w2_copy(b, t).start()
    enter(0, 0)

    def slot(k, _):
        b = lax.rem(k, 2)
        i = lax.div(k, 2)
        c = jnp.where(b == 0, i, i - 1)

        @pl.when((c >= 0) & (c < C))
        def _():
            compute(k, b, c == 0)

        @pl.when(b == 0)
        def _():
            @pl.when((i >= 2) & (i < C + 2))
            def _():
                finish1(i - 2, k - 1)

            @pl.when(i + 1 < C)
            def _():
                enter(i + 1, k + 2)

        @pl.when((b == 1) & (i < C))
        def _():
            finish0(i, k - 1, k + 2)
        return 0

    lax.fori_loop(0, 2 * C + 3, slot, 0)
    release(C - 2)
    release(C - 1)


def solution(mesh):
    S = mesh.shape['stage']

    def local(x, g, w1, w2):
        M, TL, D = x.shape
        NB = g.shape[1]
        F = w1.shape[3]
        NQ = TL // Q
        C = M * NQ
        NT1, NT2 = F // TN, D // TN
        q = Q
        bf, f32 = jnp.bfloat16, jnp.float32
        dma, reg = pltpu.SemaphoreType.DMA, pltpu.SemaphoreType.REGULAR
        any_ = pl.BlockSpec(memory_space=pl.ANY)
        vm = pl.BlockSpec(memory_space=pltpu.VMEM)
        flops = 4 * C * NB * 4 * q * D * F
        out = pl.pallas_call(
            functools.partial(_kernel, (S, NB, C, NQ, NT1, NT2, D)),
            out_shape=jax.ShapeDtypeStruct((M, TL, D), bf),
            in_specs=[any_, vm, any_, any_],
            out_specs=any_,
            scratch_shapes=[
                pltpu.VMEM((NB, NT1, D, TN), bf),
                pltpu.VMEM((NB, NT2, F, TN), bf),
                pltpu.VMEM((3, 4 * q, D), bf),
                pltpu.VMEM((4 * q, F), bf),
                pltpu.VMEM((2, 2 * q, TN), bf),
                pltpu.VMEM((2, NT2, 2 * q, TN), bf),
                pltpu.VMEM((2, q, TN), f32),
                pltpu.VMEM((2, NT2, q, TN), f32),
                pltpu.VMEM((2, NT2, q, TN), bf),
                pltpu.VMEM((3, NT2, q, TN), bf),
                pltpu.VMEM((YS, q, D), bf),
                pltpu.VMEM((2, q, D), bf),
                pltpu.VMEM((2, q, D), bf),
                dma((2, NB, max(NT1, NT2))),
                dma((3,)), dma((3,)), dma((3,)), dma((3, 3)),
                dma((2,)), dma((2, NT2)), dma((2, NT2)), dma((3, NT2)),
                dma((YS,)), dma((2,)), dma((2,)), reg,
            ],
            compiler_params=pltpu.CompilerParams(
                has_side_effects=True, vmem_limit_bytes=67043328),
            cost_estimate=pl.CostEstimate(flops=flops, bytes_accessed=2 * (2 * M * TL * D + 2 * NB * D * F),
                                          transcendentals=C * NB * 4 * q * F),
            name='stages',
        )(x, g[0].astype(f32)[:, None, :], w1[0], w2[0])
        return out[None]

    return jax.shard_map(
        local, mesh=mesh,
        in_specs=(P(None, 'tp', None), P('stage', None, None),
                  P('stage', None, None, 'tp'), P('stage', None, 'tp', None)),
        out_specs=P('stage', None, 'tp', None), check_vma=False)
```

time: 3180 us -> 1230 us (0.39)
  waiting for transfers between devices: 2150 us -> 0 us
  Pallas kernels: 0 us -> 1220 us
  matrix products: 831 us -> 0 us
  other arithmetic: 119 us -> 1.32 us
    pallas_call x0 -> x1, Pallas kernels: none -> 1220 us  [local(): pl.pallas_call(functools.partial(_kernel, (S, NB, C, NQ, NT1, NT2, D)), o...]
    reduce_scatter x22 -> x0, waiting for transfers between devices: 996 us -> none  [_block(): r = lax.psum_scatter(p, 'tp', scatter_dimension=0, tiled=True)]
    all_gather x22 -> x0, waiting for transfers between devices: 847 us -> none  [_block(): h = lax.all_gather(_ln(y, g), 'tp', axis=0, tiled=True)]
    dot_general x44 -> x0, matrix products: 831 us -> none  [the longest x22 430 us: _block(): jnp.dot(h, w1, preferred_element_type=jnp.float32)]
    ppermute x10 -> x0, waiting for transfers between devices: 309 us -> none  [local(): recv = lax.ppermute(y, 'stage', fwd)]
    reduce_sum x44 -> x0, other arithmetic: 52.2 us -> none  [the longest x22 40.1 us: _ln(): mu = jnp.mean(yf, axis=-1, keepdims=True)]
    convert_element_type x23 -> x1, other arithmetic: 35.9 us -> 1.32 us  [local(): g[0].astype(f32)[:, None, :]]
  transfers between devices with their start and end apart: 54 -> 0, of which waited for: 54 -> 0; matrix products, arithmetic and copies ran while one was open for 1% -> 0% of each run, Pallas kernels for 0% -> 0%
where the time goes in v1:
time: 1230 us
  Pallas kernels  1220 us (99%)
    pallas_call x1, Pallas kernels, local(): pl.pallas_call(functools.partial(_kernel, (S, NB, C, NQ, NT1, NT2, D)), o...  1220 us

profile of v1, /device:TPU:12, one launch (start us, length us, event | category | flops | bytes accessed | tf_op | source)
XLA Modules:
  0.0 1233.9 jit_solution(5098061302305130285)
XLA Ops:
  0.0 1.3 bitcast_convert_fusion.g_ref
  1.3 1223.9 %stages.1 = bf16[8,256,2560]{2,1,0:T(8,128)(2,1)} custom-call(bf16[8,256,2560]{2,1,0:T(8,128)(2,1)} %x_hbm.1, f32[2,1,2560]{2,1,0:T(1,128)} %bitcast_convert_fusion.g_ref, bf16[2,2560,2560]{2,1,0:T(8,128)(2,1)} %bitcast.7, bf16[2,2560,2560]{2,1,0:T(8,128)(2,1)} %bitcast.8), custom_call_target="tpu_custom_call" | custom-call | flops 429496729600 | bytes 73400320 | tf_op jit(solution)/shard_map/stages/pallas_call | solution.py:262
  1225.2 8.7 copy.8

commit v2 on v1

v2 whole, which is shorter than its diff:
```python
import functools

import jax
import jax.numpy as jnp
from jax import lax
from jax.experimental import pallas as pl
from jax.experimental.pallas import tpu as pltpu
from jax.sharding import PartitionSpec as P

EPS = 1e-5
Q = 32
TN = 512
YS = 4
RS = 4
RB = 16
MESH = pl.DeviceIdType.MESH


def _kernel(cfg, x_hbm, g_ref, w1_hbm, w2_hbm, y_hbm, xc_hbm,
            w1s, w2s, h, a, psend, precv, keep, ssend, srecv, y0, y1, yout,
            w_sem, h_send, h_recv, p_send, p_recv, s_send, s_recv,
            yin_sem, ysend_sem, yhbm_sem, xs_send, xs_recv, credit):
    S, NB, C, NQ, NT1, NT2, D = cfg
    q = Q
    s = lax.axis_index('stage')
    r = lax.axis_index('tp')
    xr = lax.div(r, 2)
    cr = lax.rem(r, 2)
    partner = xr * 2 + (1 - cr)
    cross = (1 - xr) * 2 + cr
    first_stage, last_stage = s == 0, s == S - 1


    def w1_copy(b, t):
        return pltpu.make_async_copy(w1_hbm.at[b, :, pl.ds(t * TN, TN)], w1s.at[b, t], w_sem.at[0, b, t])

    def w2_copy(b, t):
        return pltpu.make_async_copy(w2_hbm.at[b, :, pl.ds(t * TN, TN)], w2s.at[b, t], w_sem.at[1, b, t])

    def remote(src, dst, ss, rs, **dev):
        return pltpu.make_async_remote_copy(src_ref=src, dst_ref=dst, send_sem=ss, recv_sem=rs,
                                            device_id=dev, device_id_type=MESH)

    def h_copy(b):
        return remote(h.at[b, pl.ds(0, 2 * q)], h.at[b, pl.ds(2 * q, 2 * q)],
                      h_send.at[b], h_recv.at[b], tp=partner)

    def p_copy(b, t):
        return remote(psend.at[t % 2], precv.at[b, t], p_send.at[t % 2], p_recv.at[b, t], tp=partner)

    def s_copy(b, c, t):
        e, i, k = lax.rem(c, 2), lax.rem(c, RS), (2 - b) * q
        return remote(ssend.at[b, e, t, pl.ds(0, k)], srecv.at[b, i, t, pl.ds(0, k)],
                      s_send.at[b, e, t], s_recv.at[b, i, t], tp=cross)

    def hbm_rows(ref, c):
        return ref.at[lax.div(c, NQ), pl.ds(pl.multiple_of(lax.rem(c, NQ) * q, q), q)]

    def x_send(c):
        return pltpu.make_async_remote_copy(
            src_ref=hbm_rows(x_hbm, c), dst_ref=hbm_rows(xc_hbm, c),
            send_sem=xs_send.at[c], recv_sem=xs_recv.at[c],
            device_id={'stage': jnp.int32(0), 'tp': cross}, device_id_type=MESH)

    def x_copy(c, part):
        i = lax.rem(c, YS)
        src = x_hbm if part == 0 else xc_hbm
        return pltpu.make_async_copy(hbm_rows(src, c), y0.at[i, pl.ds(part * q, q)], yin_sem.at[i, part])

    def y_next(c, part):
        i, o = lax.rem(c, YS), lax.rem(c, 2)
        return remote(yout.at[o], y0.at[i, pl.ds(part * q, q)], ysend_sem.at[o, part], yin_sem.at[i, part],
                      stage=s + 1, tp=r if part == 0 else cross)

    def y_store(c):
        o = lax.rem(c, 2)
        return pltpu.make_async_copy(yout.at[o], hbm_rows(y_hbm, c), yhbm_sem.at[o])

    def norm(yf, b):
        mu = jnp.mean(yf, axis=-1, keepdims=True)
        d = yf - mu
        var = jnp.mean(jnp.square(d), axis=-1, keepdims=True)
        return (d * lax.rsqrt(var + EPS) * g_ref[b]).astype(jnp.bfloat16)

    def fetch(c):
        x_send(c).wait_recv()
        x_copy(c, 0).start()
        x_copy(c, 1).start()

    def enter(c):
        i = lax.rem(c, YS)

        @pl.when(first_stage)
        def _():
            x_copy(c, 0).wait()
            x_copy(c, 1).wait()

            @pl.when(c + 2 < C)
            def _():
                fetch(c + 2)

        @pl.when(jnp.logical_not(first_stage))
        def _():
            y_next(c, 0).wait_recv()
            y_next(c, 1).wait_recv()

        for u in range(2 * q // RB):
            rr = slice(u * RB, (u + 1) * RB)
            h[0, rr] = norm(y0[i, rr].astype(jnp.float32), 0)
        h_copy(0).start()

    def add_up(y, b, c, lo):
        e, i = lax.rem(c, 2), lax.rem(c, RS)
        mine = slice((lo + q) % (2 * q), (lo + q) % (2 * q) + RB)
        theirs = slice(lo, lo + RB)
        parts = []
        for t in range(NT2):
            parts.append((y[:, t * TN:(t + 1) * TN].astype(jnp.float32)
                          + (ssend[b, e, t, mine].astype(jnp.float32)
                             + srecv[b, i, t, theirs].astype(jnp.float32))).astype(jnp.bfloat16))
        return jnp.concatenate(parts, axis=-1)

    def finish0(c):
        for t in range(NT2):
            s_copy(0, c, t).wait()
        i, o = lax.rem(c, YS), lax.rem(c, 2)
        for u in range(2 * q // RB):
            rr = slice(u * RB, (u + 1) * RB)
            y = add_up(y0[i, rr], 0, c, u * RB)
            if u * RB < q:
                y1[o, rr] = y
            h[1, rr] = norm(y.astype(jnp.float32), 1)
        h_copy(1).start()

        @pl.when((s > 0) & (c + YS < C))
        def _():
            pl.semaphore_signal(credit.at[0], inc=1, device_id={'stage': s - 1, 'tp': r}, device_id_type=MESH)
            pl.semaphore_signal(credit.at[1], inc=1, device_id={'stage': s - 1, 'tp': cross},
                                device_id_type=MESH)

    def release(c):
        y_store(c).wait()

        @pl.when(s < S - 1)
        def _():
            y_next(c, 1).wait_send()
            y_next(c, 0).wait_send()

    def finish1(c):
        o = lax.rem(c, 2)

        @pl.when(c >= 2)
        def _():
            release(c - 2)
        for t in range(NT2):
            s_copy(1, c, t).wait()
        for u in range(q // RB):
            rr = slice(u * RB, (u + 1) * RB)
            yout[o, rr] = add_up(y1[o, rr], 1, c, u * RB)

        @pl.when(s < S - 1)
        def _():
            @pl.when(c >= YS)
            def _():
                pl.semaphore_wait(credit.at[0], 1)
                pl.semaphore_wait(credit.at[1], 1)
            y_next(c, 1).start()
            y_next(c, 0).start()
        y_store(c).start()

    def combine(b, c, t):
        e = lax.rem(c, 2)
        p_copy(b, t).wait()
        ssend[b, e, t, 0:q] = (keep[t % 2, q:2 * q] + precv[b, t, q:2 * q].astype(jnp.float32)
                               ).astype(jnp.bfloat16)
        ssend[b, e, t, q:2 * q] = (keep[t % 2, 0:q] + precv[b, t, 0:q].astype(jnp.float32)
                                   ).astype(jnp.bfloat16)
        s_copy(b, c, t).start()

    def compute(b, c):
        @pl.when(c == 0)
        def _():
            for t in range(NT1):
                w1_copy(b, t).wait()
        h_copy(b).wait()
        for t in range(NT1):
            u = jnp.dot(h[b], w1s[b, t], preferred_element_type=jnp.float32)
            a[:, t * TN:(t + 1) * TN] = jax.nn.gelu(u).astype(jnp.bfloat16)

        @pl.when(c == 0)
        def _():
            for t in range(NT2):
                w2_copy(b, t).wait()
        for t in range(NT2):
            p = jnp.dot(a[...], w2s[b, t], preferred_element_type=jnp.float32)
            psend[t % 2] = p[2 * q:].astype(jnp.bfloat16)
            keep[t % 2] = p[0:2 * q]
            p_copy(b, t).start()
            if t > 0:
                combine(b, c, t - 1)

    @pl.when(last_stage)
    def _():
        def send(c, _):
            x_send(c).start()
            return 0
        lax.fori_loop(0, C, send, 0)

    for b in range(NB):
        for t in range(NT1):
            w1_copy(b, t).start()
        for t in range(NT2):
            w2_copy(b, t).start()

    @pl.when(first_stage)
    def _():
        fetch(0)
        fetch(1)
    enter(0)

    def step(i, _):
        @pl.when(i < C)
        def _():
            compute(0, i)

        @pl.when((i >= 1) & (i <= C))
        def _():
            finish0(i - 1)

        @pl.when(i >= 2)
        def _():
            finish1(i - 2)

        @pl.when(i < C)
        def _():
            combine(0, i, NT2 - 1)

        @pl.when((i >= 1) & (i <= C))
        def _():
            compute(1, i - 1)

        @pl.when(i + 1 < C)
        def _():
            enter(i + 1)

        @pl.when((i >= 1) & (i <= C))
        def _():
            combine(1, i - 1, NT2 - 1)
        return 0

    lax.fori_loop(0, C + 2, step, 0)
    release(C - 2)
    release(C - 1)

    @pl.when(last_stage)
    def _():
        def sent(c, _):
            x_send(c).wait_send()
            return 0
        lax.fori_loop(0, C, sent, 0)


def solution(mesh):
    S = mesh.shape['stage']

    def local(x, g, w1, w2):
        M, TL, D = x.shape
        NB = g.shape[1]
        F = w1.shape[3]
        NQ = TL // Q
        C = M * NQ
        NT1, NT2 = F // TN, D // TN
        q = Q
        bf, f32 = jnp.bfloat16, jnp.float32
        dma, reg = pltpu.SemaphoreType.DMA, pltpu.SemaphoreType.REGULAR
        any_ = pl.BlockSpec(memory_space=pl.ANY)
        vm = pl.BlockSpec(memory_space=pltpu.VMEM)
        flops = 4 * C * NB * 4 * q * D * F
        out, _ = pl.pallas_call(
            functools.partial(_kernel, (S, NB, C, NQ, NT1, NT2, D)),
            out_shape=(jax.ShapeDtypeStruct((M, TL, D), bf), jax.ShapeDtypeStruct((M, TL, D), bf)),
            in_specs=[any_, vm, any_, any_],
            out_specs=(any_, any_),
            scratch_shapes=[
                pltpu.VMEM((NB, NT1, D, TN), bf),
                pltpu.VMEM((NB, NT2, F, TN), bf),
                pltpu.VMEM((NB, 4 * q, D), bf),
                pltpu.VMEM((4 * q, F), bf),
                pltpu.VMEM((2, 2 * q, TN), bf),
                pltpu.VMEM((NB, NT2, 2 * q, TN), bf),
                pltpu.VMEM((2, 2 * q, TN), f32),
                pltpu.VMEM((NB, 2, NT2, 2 * q, TN), bf),
                pltpu.VMEM((NB, RS, NT2, 2 * q, TN), bf),
                pltpu.VMEM((YS, 2 * q, D), bf),
                pltpu.VMEM((2, q, D), bf),
                pltpu.VMEM((2, q, D), bf),
                dma((2, NB, max(NT1, NT2))),
                dma((NB,)), dma((NB,)),
                dma((2,)), dma((NB, NT2)), dma((NB, 2, NT2)), dma((NB, RS, NT2)),
                dma((YS, 2)), dma((2, 2)), dma((2,)), dma((C,)), dma((C,)), reg((2,)),
            ],
            compiler_params=pltpu.CompilerParams(
                has_side_effects=True, vmem_limit_bytes=67043328),
            cost_estimate=pl.CostEstimate(flops=flops, bytes_accessed=2 * (2 * M * TL * D + 2 * NB * D * F),
                                          transcendentals=C * NB * 4 * q * F),
            name='stages',
        )(x, g[0].astype(f32)[:, None, :], w1[0], w2[0])
        return out[None]

    return jax.shard_map(
        local, mesh=mesh,
        in_specs=(P(None, 'tp', None), P('stage', None, None),
                  P('stage', None, None, 'tp'), P('stage', None, 'tp', None)),
        out_specs=P('stage', None, 'tp', None), check_vma=False)
```

time: 1230 us -> 1170 us (0.951)
  Pallas kernels: 1220 us -> 1160 us
    pallas_call x1, Pallas kernels: 1220 us -> 1160 us  [local(): pl.pallas_call(functools.partial(_kernel, (S, NB, C, NQ, NT1, NT2, D)), o...]
where the time goes in v2:
time: 1170 us
  Pallas kernels  1160 us (99%)
    pallas_call x1, Pallas kernels, local(): pl.pallas_call(functools.partial(_kernel, (S, NB, C, NQ, NT1, NT2, D)), o...  1160 us

profile of v2, /device:TPU:12, one launch (start us, length us, event | category | flops | bytes accessed | tf_op | source)
XLA Modules:
  0.0 1169.1 jit_solution(3640083828560791987)
XLA Ops:
  0.0 1.3 bitcast_convert_fusion.g_ref
  1.3 1159.0 %stages.1 = (bf16[8,256,2560]{2,1,0:T(8,128)(2,1)}, bf16[8,256,2560]{2,1,0:T(8,128)(2,1)}) custom-call(bf16[8,256,2560]{2,1,0:T(8,128)(2,1)} %x_hbm.1, f32[2,1,2560]{2,1,0:T(1,128)} %bitcast_convert_fusion.g_ref, bf16[2,2560,2560]{2,1,0:T(8,128)(2,1)} %bitcast.7, bf16[2,2560,2560]{2,1,0:T(8,128)(2,1)} %bitcast.8), custom_call_target="tpu_custom_call" | custom-call | flops 429496729600 | bytes 73400320 | tf_op jit(solution)/shard_map/stages/pallas_call | solution.py:279
  1160.4 8.7 copy.8

commit v3 on v2

--- a/solution.py
+++ b/solution.py
@@ -12,6 +12,7 @@
 TN = 512
 YS = 4
 RS = 4
+T0 = 3
 RB = 16
 MESH = pl.DeviceIdType.MESH
 
@@ -28,7 +29,7 @@
     cr = lax.rem(r, 2)
     partner = xr * 2 + (1 - cr)
     cross = (1 - xr) * 2 + cr
-    first_stage, last_stage = s == 0, s == S - 1
+    first_stage = s == 0
 
 
     def w1_copy(b, t):
@@ -46,7 +47,7 @@
                       h_send.at[b], h_recv.at[b], tp=partner)
 
     def p_copy(b, t):
-        return remote(psend.at[t % 2], precv.at[b, t], p_send.at[t % 2], p_recv.at[b, t], tp=partner)
+        return remote(psend.at[t], precv.at[b, t], p_send.at[t], p_recv.at[b, t], tp=partner)
 
     def s_copy(b, c, t):
         e, i, k = lax.rem(c, 2), lax.rem(c, RS), (2 - b) * q
@@ -171,9 +172,9 @@
     def combine(b, c, t):
         e = lax.rem(c, 2)
         p_copy(b, t).wait()
-        ssend[b, e, t, 0:q] = (keep[t % 2, q:2 * q] + precv[b, t, q:2 * q].astype(jnp.float32)
+        ssend[b, e, t, 0:q] = (keep[t, q:2 * q] + precv[b, t, q:2 * q].astype(jnp.float32)
                                ).astype(jnp.bfloat16)
-        ssend[b, e, t, q:2 * q] = (keep[t % 2, 0:q] + precv[b, t, 0:q].astype(jnp.float32)
+        ssend[b, e, t, q:2 * q] = (keep[t, 0:q] + precv[b, t, 0:q].astype(jnp.float32)
                                    ).astype(jnp.bfloat16)
         s_copy(b, c, t).start()
 
@@ -193,18 +194,26 @@
                 w2_copy(b, t).wait()
         for t in range(NT2):
             p = jnp.dot(a[...], w2s[b, t], preferred_element_type=jnp.float32)
-            psend[t % 2] = p[2 * q:].astype(jnp.bfloat16)
-            keep[t % 2] = p[0:2 * q]
-            p_copy(b, t).start()
-            if t > 0:
-                combine(b, c, t - 1)
-
-    @pl.when(last_stage)
-    def _():
-        def send(c, _):
+            psend[t] = p[2 * q:].astype(jnp.bfloat16)
+            keep[t] = p[0:2 * q]
+            if t == T0 - 1:
+                for v in range(T0):
+                    p_copy(b, v).start()
+        for v in range(T0, NT2):
+            p_copy(b, v).start()
+        for v in range(T0):
+            combine(b, c, v)
+
+    def x_mine(c):
+        src = jnp.where(c < 36, 1 + lax.rem(c, 3), jnp.where(lax.rem(c - 36, 14) < 5, 2, 3))
+        return s == src
+
+    def send(c, _):
+        @pl.when(x_mine(c))
+        def _():
             x_send(c).start()
-            return 0
-        lax.fori_loop(0, C, send, 0)
+        return 0
+    lax.fori_loop(0, C, send, 0)
 
     for b in range(NB):
         for t in range(NT1):
@@ -233,7 +242,8 @@
 
         @pl.when(i < C)
         def _():
-            combine(0, i, NT2 - 1)
+            for t in range(T0, NT2):
+                combine(0, i, t)
 
         @pl.when((i >= 1) & (i <= C))
         def _():
@@ -245,19 +255,20 @@
 
         @pl.when((i >= 1) & (i <= C))
         def _():
-            combine(1, i - 1, NT2 - 1)
+            for t in range(T0, NT2):
+                combine(1, i - 1, t)
         return 0
 
     lax.fori_loop(0, C + 2, step, 0)
     release(C - 2)
     release(C - 1)
 
-    @pl.when(last_stage)
-    def _():
-        def sent(c, _):
+    def sent(c, _):
+        @pl.when(x_mine(c))
+        def _():
             x_send(c).wait_send()
-            return 0
-        lax.fori_loop(0, C, sent, 0)
+        return 0
+    lax.fori_loop(0, C, sent, 0)
 
 
 def solution(mesh):
@@ -286,9 +297,9 @@
                 pltpu.VMEM((NB, NT2, F, TN), bf),
                 pltpu.VMEM((NB, 4 * q, D), bf),
                 pltpu.VMEM((4 * q, F), bf),
-                pltpu.VMEM((2, 2 * q, TN), bf),
+                pltpu.VMEM((NT2, 2 * q, TN), bf),
                 pltpu.VMEM((NB, NT2, 2 * q, TN), bf),
-                pltpu.VMEM((2, 2 * q, TN), f32),
+                pltpu.VMEM((NT2, 2 * q, TN), f32),
                 pltpu.VMEM((NB, 2, NT2, 2 * q, TN), bf),
                 pltpu.VMEM((NB, RS, NT2, 2 * q, TN), bf),
                 pltpu.VMEM((YS, 2 * q, D), bf),
@@ -296,7 +307,7 @@
                 pltpu.VMEM((2, q, D), bf),
                 dma((2, NB, max(NT1, NT2))),
                 dma((NB,)), dma((NB,)),
-                dma((2,)), dma((NB, NT2)), dma((NB, 2, NT2)), dma((NB, RS, NT2)),
+                dma((NT2,)), dma((NB, NT2)), dma((NB, 2, NT2)), dma((NB, RS, NT2)),
                 dma((YS, 2)), dma((2, 2)), dma((2,)), dma((C,)), dma((C,)), reg((2,)),
             ],
             compiler_params=pltpu.CompilerParams(

time: 1170 us -> 1110 us (0.949)
  Pallas kernels: 1160 us -> 1100 us
    pallas_call x1, Pallas kernels: 1160 us -> 1100 us  [local(): pl.pallas_call(functools.partial(_kernel, (S, NB, C, NQ, NT1, NT2, D)), o...]
where the time goes in v3:
time: 1110 us
  Pallas kernels  1100 us (99%)
    pallas_call x1, Pallas kernels, local(): pl.pallas_call(functools.partial(_kernel, (S, NB, C, NQ, NT1, NT2, D)), o...  1100 us

profile of v3, /device:TPU:12, one launch (start us, length us, event | category | flops | bytes accessed | tf_op | source)
XLA Modules:
  0.0 1113.9 jit_solution(6106735097748905712)
XLA Ops:
  0.0 1.3 bitcast_convert_fusion.g_ref
  1.3 1103.8 %stages.1 = (bf16[8,256,2560]{2,1,0:T(8,128)(2,1)}, bf16[8,256,2560]{2,1,0:T(8,128)(2,1)}) custom-call(bf16[8,256,2560]{2,1,0:T(8,128)(2,1)} %x_hbm.1, f32[2,1,2560]{2,1,0:T(1,128)} %bitcast_convert_fusion.g_ref, bf16[2,2560,2560]{2,1,0:T(8,128)(2,1)} %bitcast.7, bf16[2,2560,2560]{2,1,0:T(8,128)(2,1)} %bitcast.8), custom_call_target="tpu_custom_call" | custom-call | flops 429496729600 | bytes 73400320 | tf_op jit(solution)/shard_map/stages/pallas_call | solution.py:290
  1105.2 8.7 copy.8
